TPU v7x, 32 devices: a whole 2x2x4 slice. The times are simulated.
32 devices in a mesh: frame: 8 (over y, x, core), row: 4 (over z).
Axes of the slice: x: 2, y: 2, z: 4, core: 2. Of those that a mesh axis runs over, the one named last changes fastest.
Arguments:
- tokens: bfloat16 [8, 512, 2048], P('frame', 'row'), may hold values from -6 to 6
- w_gate: bfloat16 [2048, 4096], P(None, 'row'), may hold values from -0.125 to 0.125
- w_value: bfloat16 [2048, 4096], P(None, 'row'), may hold values from -0.125 to 0.125
- w_state_proj: bfloat16 [2048, 512], replicated, may hold values from -0.03125 to 0.03125
- w_step: bfloat16 [2, 2048, 64], P(None, None, 'row'), may hold values from -0.125 to 0.125
- step_bias: float32 [2, 64], P(None, 'row'), may hold values from -3 to 0
- decay_rate: float32 [2, 64], P(None, 'row'), may hold values from 0 to 0.3, as said below
- conv_taps: float32 [2, 4, 4096], P(None, None, 'row'), may hold values from -3 to 3
- skip_gain: float32 [2, 64], P(None, 'row'), may hold values from 0.1 to 16, as said below
- norm_gain: float32 [4096], P('row'), may hold values from 0.1 to 1.9
- w_out: bfloat16 [4096, 2048], P('row'), may hold values from -0.09375 to 0.09375
Outputs:
- mixed: bfloat16 [8, 512, 2048], P('frame', 'row')
Inputs may be any that keep to these rules, and one draw needn't show every extreme that they name: `decay_rate`: positive decay rates. `skip_gain`: positive skip weights.
All inputs are finite; a program needn't handle non-finite values.
Results may differ from a plain program's by a relative error of at most 0.015.
Values may be sent and summed in bfloat16 or wider, within the bound.
No kernel may reach another device: no remote copies, remote signals or barrier semaphores. Data moves between devices by JAX's collectives and lax.ppermute only.
A program may use at most 128 MiB of HBM per device.

v0:
```python
import jax
import jax.numpy as jnp
from jax import lax
from jax.sharding import PartitionSpec as P

D_INNER = 4096
HEAD_DIM = 64
CONV = 4
BLK = 128


def with_halo(shard, sides, width):
    for axis, dim in sides:
        devices, length = (lax.axis_size(axis), shard.shape[dim])
        up = [(i, (i + 1) % devices) for i in range(devices - 1)]
        down = [(j, i) for i, j in up]
        last = lax.slice_in_dim(shard, length - width, length, axis=dim)
        initial = lax.slice_in_dim(shard, 0, width, axis=dim)
        before = lax.ppermute(last, axis, up)
        after = lax.ppermute(initial, axis, down)
        shard = jnp.concatenate([before, shard, after], axis=dim)
    return shard


def carried_in(shard, axis, combine, identity, reverse):
    devices, mine = (lax.axis_size(axis), lax.axis_index(axis))
    everything = jax.tree.map(
        lambda part, kind: lax.all_gather(part.astype(kind), axis),
        shard,
        (jnp.bfloat16, jnp.bfloat16),
    )
    start = jax.tree.map(
        lambda part, zero: jnp.broadcast_to(jnp.asarray(zero, part.dtype), part.shape),
        shard,
        identity,
    )

    def lap(k, before):
        at = devices - 1 - k if reverse else k
        reached = at > mine if reverse else at < mine
        new = combine(
            before, jax.tree.map(lambda part, own: part[at].astype(own.dtype), everything, shard)
        )
        return jax.tree.map(lambda a, b: jnp.where(reached, a, b), new, before)

    return lax.fori_loop(0, devices, lap, start)


def block_weights(scores, log_cum, dt_block):
    size = scores.shape[0]
    row_index = lax.broadcasted_iota(jnp.int32, (size, size), 0)
    col_index = lax.broadcasted_iota(jnp.int32, (size, size), 1)
    causal = row_index >= col_index
    log_gap = log_cum.T[:, :, None] - log_cum.T[:, None, :]
    fading = jnp.exp(jnp.where(causal[None], log_gap, -jnp.inf))
    return (scores[None] * fading * dt_block.T[:, None, :]).astype(jnp.bfloat16)


def local_pass(values, b_rows, c_rows, dt_rows, rate_row):
    tok_count, heads_here, head_width = values.shape
    block_count = tok_count // BLK
    blocks = (
        values.reshape(block_count, BLK, heads_here, head_width),
        b_rows.reshape(block_count, BLK, -1),
        c_rows.reshape(block_count, BLK, -1),
        dt_rows.reshape(block_count, BLK, heads_here),
    )
    state_zero = jnp.zeros((heads_here, head_width, b_rows.shape[1]), jnp.float32)

    def advance(carry, block):
        carry_state, offset = carry
        x_block, b_block, c_block, dt_block = block
        log_cum = jnp.cumsum(-dt_block * rate_row[None, :], axis=0)
        scores = jnp.einsum("tn,sn->ts", c_block, b_block, preferred_element_type=jnp.float32)
        weights = block_weights(scores, log_cum, dt_block)
        inner_out = jnp.einsum("hts,shp->thp", weights, x_block, preferred_element_type=jnp.float32)
        log_last = log_cum[-1]
        carried = (
            (jnp.exp(log_last[None, :] - log_cum) * dt_block)[:, :, None]
            * x_block.astype(jnp.float32)
        ).astype(jnp.bfloat16)
        update = jnp.einsum("sn,shp->hpn", b_block, carried, preferred_element_type=jnp.float32)
        new_state = jnp.exp(log_last)[:, None, None] * carry_state + update
        return ((new_state, offset + log_last), (inner_out, log_cum, carry_state, offset))

    finals, saved = lax.scan(advance, (state_zero, jnp.zeros((heads_here,), jnp.float32)), blocks)
    return (finals, saved, blocks)


def finish(saved, blocks, incoming, skip_row):
    inner_out, log_cum, starts, offsets = saved
    x_blocks, unused_b, c_blocks, unused_dt = blocks
    entering = (starts + jnp.exp(offsets)[:, :, None, None] * incoming[None]).astype(jnp.bfloat16)
    carried_out = jnp.einsum(
        "btn,bhpn->bthp", c_blocks, entering, preferred_element_type=jnp.float32
    )
    result = (
        inner_out
        + carried_out * jnp.exp(log_cum)[..., None]
        + skip_row[None, None, :, None] * x_blocks.astype(jnp.float32)
    )
    return result.reshape(-1, result.shape[2], result.shape[3])


def chain_link(earlier, later):
    return (earlier[0] + later[0], jnp.exp(later[0])[:, None, None] * earlier[1] + later[1])


def conv_pass(padded, taps, tok_count, backward):
    reach = taps.shape[0] - 1
    running = jnp.zeros((tok_count, padded.shape[1]), jnp.float32)
    for tap_index in range(taps.shape[0]):
        first_row = 2 * reach - tap_index if backward else tap_index
        running = running + taps[tap_index][None, :] * padded[first_row : first_row + tok_count]
    return jax.nn.silu(running).astype(jnp.bfloat16)


def per_device(
    tokens,
    w_gate,
    w_value,
    w_state_proj,
    w_step,
    step_bias,
    decay_rate,
    conv_taps,
    skip_gain,
    norm_gain,
    w_out,
):
    channels = w_gate.shape[1]
    heads_here = step_bias.shape[1]
    state_size = w_state_proj.shape[1] // 4
    shard_piece = lax.all_gather(tokens, "row", axis=1, tiled=True)
    matrices = (w_gate, w_value, w_state_proj, w_step[0], w_step[1])
    outputs = [
        jnp.einsum("frd,dk->frk", shard_piece, matrix, preferred_element_type=jnp.float32).astype(
            jnp.bfloat16
        )
        for matrix in matrices
    ]
    projected = jnp.concatenate(outputs, axis=2)
    frame_count, patch_count = (projected.shape[0], projected.shape[1])
    tok_count = frame_count * patch_count
    projected = projected.reshape(tok_count, -1)
    gate_in = projected[:, :channels]
    x_raw = projected[:, channels : 2 * channels]
    edge = 2 * channels + 4 * state_size
    bc_cols = projected[:, 2 * channels : edge]
    dt_forward = jax.nn.softplus(
        projected[:, edge : edge + heads_here].astype(jnp.float32) + step_bias[0][None, :]
    )
    dt_backward = jax.nn.softplus(
        projected[:, edge + heads_here : edge + 2 * heads_here].astype(jnp.float32)
        + step_bias[1][None, :]
    )
    padded = with_halo(x_raw, (("frame", 0),), CONV - 1).astype(jnp.float32)
    shape_heads = (tok_count, heads_here, HEAD_DIM)
    x_forward = conv_pass(padded, conv_taps[0], tok_count, False).reshape(shape_heads)
    x_backward = conv_pass(padded, conv_taps[1], tok_count, True).reshape(shape_heads)
    finals_fwd, saved_fwd, blocks_fwd = local_pass(
        x_forward,
        bc_cols[:, :state_size],
        bc_cols[:, state_size : 2 * state_size],
        dt_forward,
        decay_rate[0],
    )
    finals_bwd, saved_bwd, blocks_bwd = local_pass(
        jnp.flip(x_backward, 0),
        jnp.flip(bc_cols[:, 2 * state_size : 3 * state_size], 0),
        jnp.flip(bc_cols[:, 3 * state_size :], 0),
        jnp.flip(dt_backward, 0),
        decay_rate[1],
    )
    empty_pair = (
        jnp.zeros((heads_here,), jnp.float32),
        jnp.zeros((heads_here, HEAD_DIM, state_size), jnp.float32),
    )
    entry_fwd = carried_in((finals_fwd[1], finals_fwd[0]), "frame", chain_link, empty_pair, False)[
        1
    ]
    entry_bwd = carried_in((finals_bwd[1], finals_bwd[0]), "frame", chain_link, empty_pair, True)[1]
    y_forward = finish(saved_fwd, blocks_fwd, entry_fwd, skip_gain[0])
    y_backward = jnp.flip(finish(saved_bwd, blocks_bwd, entry_bwd, skip_gain[1]), 0)
    summed = (y_forward + y_backward).reshape(tok_count, channels)
    gated = summed * jax.nn.silu(gate_in.astype(jnp.float32))
    local_squares = jnp.sum(gated * gated, axis=-1)
    total_squares = lax.psum(local_squares, "row")
    scale = lax.rsqrt(total_squares / D_INNER + 1e-05)
    normed = (gated * scale[:, None] * norm_gain[None, :]).astype(jnp.bfloat16)
    normed = normed.reshape(frame_count, patch_count, channels)
    partial_value = jnp.einsum("fpc,cd->fpd", normed, w_out, preferred_element_type=jnp.float32)
    reduced = lax.psum_scatter(
        jnp.transpose(partial_value, (1, 0, 2)).astype(jnp.bfloat16),
        "row",
        scatter_dimension=0,
        tiled=True,
    ).astype(jnp.float32)
    mixed = jnp.transpose(reduced, (1, 0, 2)).astype(jnp.bfloat16)
    return mixed


def solution(mesh):
    return jax.shard_map(
        per_device,
        mesh=mesh,
        in_specs=(
            P("frame", "row", None),
            P(None, "row"),
            P(None, "row"),
            P(),
            P(None, None, "row"),
            P(None, "row"),
            P(None, "row"),
            P(None, None, "row"),
            P(None, "row"),
            P("row"),
            P("row", None),
        ),
        out_specs=P("frame", "row", None),
        check_vma=False,
    )
```

profile of v0, /device:TPU:0, one launch (start us, length us, event | category | flops | bytes accessed | tf_op | source)
XLA Modules:
  0.0 298.6 jit_solution(7827594384585309129)
XLA Ops:
  11.0 46.3 %all-gather.8.cloned.1.call-done = bf16[1,512,2048]{2,1,0:T(8,128)(2,1)} async-done(((bf16[1,128,2048]{2,1,0:T(8,128)(2,1)}), bf16[1,512,2048]{2,1,0:T(8,128)(2,1)}) %all-gather.8.cloned.1.call-update) | async-done | bytes 2097168 | tf_op jit(solution)/shard_map/all_gather | solution.py:134
  57.3 5.3 %fusion.94 = bf16[1,512,2592]{1,2,0:T(8,128)(2,1)S(1)} fusion(bf16[2048,1024]{1,0:T(8,128)(2,1)} %param.20, bf16[1,512,2048]{2,1,0:T(8,128)(2,1)} %all-gather.8.cloned.1.call-done), kind=kOutput, calls=%fused_computation.129 | convolution fusion | flops 2148007936 | bytes 7340032 | tf_op jit(solution)/shard_map/frd,dk->frk/dot_general | solution.py:137
  62.7 2.4 fusion.88
  70.8 3.7 %collective-permute-start = (bf16[3,1024]{0,1:T(8,128)(2,1)}, bf16[3,1024]{0,1:T(8,128)(2,1)}, u32[]{:S(2)}, u32[]{:S(2)}) collective-permute-start(bf16[3,1024]{0,1:T(8,128)(2,1)} %get-tuple-element.661), channel_id=1, source_target_pairs={{0,4},{4,8},{8,12},{12,16},{16,20},{20,24},{24,28},{1,5},{5,9},{9,... | collective-permute-start | bytes 18440 | tf_op jit(solution)/shard_map/ppermute | solution.py:19
  86.2 5.8 %multiply_convert_fusion.8 = (bf16[512,1024]{0,1:T(8,128)(2,1)}, bf16[512,1024]{0,1:T(8,128)(2,1)}) fusion(f32[518,1024]{0,1:T(8,128)S(1)} %maximum_convert_fusion, f32[1024]{0:T(1024)S(1)} %bitcast.313, f32[1024]{0:T(1024)S(1)} %bitcast.314, f32[1024]{0:T(1024)S(1)} %bitcast.315, f32[1024]{0:T(1024)S(1)} %bitcast.310, f32[1024]{0:T(1024)S(1)} %bitcast.316, ...), kind=kLoop, calls=%fused_computation.123 | loop fusion | flops 12582912 | bytes 16809984 | tf_op jit(solution)/shard_map/convert_element_type | solution.py:115
  92.0 3.7 %rev.20 = bf16[512,16,64]{0,2,1:T(8,128)(2,1)} reverse(bf16[512,16,64]{0,2,1:T(8,128)(2,1)} %bitcast.297), dimensions={0} | reverse | bytes 2097152 | tf_op jit(solution)/shard_map/jit(_flip)/rev | solution.py:169
  95.6 2.5 copy_bitcast_fusion.1
  102.6 44.9 %while.74 = (s32[]{:T(128)}, f32[16,64,128]{2,1,0:T(8,128)S(1)}, f32[16]{0:T(128)}, f32[4,128,16,64]{1,3,2,0:T(8,128)}, f32[4,128,16]{2,1,0:T(8,128)}, /*index=5...) while((s32[]{:T(128)}, f32[16,64,128]{2,1,0:T(8,128)S(1)}, ...), condition=%wide.region_7.8_spmd.clone, body=%wide.region_5.7_spmd.clone.sunk | while | flops 73816096 | bytes 3641788 | solution.py:86
  120.5 2.3 fusion.185
  131.9 2.3 fusion.185
  143.3 2.4 fusion.185
  149.6 2.5 copy.82
  156.3 23.3 %while.72 = (s32[]{:T(128)}, f32[16,64,128]{2,1,0:T(8,128)S(1)}, f32[16]{0:T(128)S(1)}, f32[4,128,16,64]{1,3,2,0:T(8,128)}, f32[4,128,16]{2,1,0:T(8,128)S(1)}, /...) while((s32[]{:T(128)}, f32[16,64,128]{2,1,0:T(8,128)S(1)}, ...), condition=%wide.region_2.3_spmd.clone, body=%wide.region_0.2_spmd.clone.sunk | while | flops 73816096 | bytes 3699580 | solution.py:86
  177.2 2.3 fusion.175
  184.7 13.4 %all-reduce.2 = (bf16[128]{0:T(256)(128)(2,1)S(1)}, bf16[128]{0:T(256)(128)(2,1)S(1)}) all-reduce(bf16[128]{0:T(256)(128)(2,1)S(1)} %dynamic-update-slice.1, bf16[128]{0:T(256)(128)(2,1)S(1)} %dynamic-update-slice), channel_id=4, replica_groups=mesh['frame'=8,'row'=4] {'frame'}, use_global_device_ids=true, to_apply=%add.1 | all-reduce | flops 256 | bytes 1024
  199.4 9.2 %while.75 = (s32[]{:T(128)}, f32[16,64,128]{2,1,0:T(8,128)S(1)}, s32[]{:T(128)}, bf16[8,16]{1,0:T(8,128)(2,1)S(1)}, bf16[8,16,64,128]{3,2,1,0:T(8,128)(2,1)}, /*index=5*/s32[]{:T(128)}, s32[]{:T(128)}, s32[]{:T(128)}, s32[]{:T(128)}) while((s32[]{:T(128)}, f32[16,64,128]{2,1,0:T(8,128)S(1)}, s32[]{:T(128)}, ...), condition=%wide.region_9.10_spmd.clone, body=%wide.region_8.9_spmd.clone.sunk | while | flops 655384 | bytes 1311055 | solution.py:46
  208.6 3.1 %add_bitcast_fusion = f32[4,16,8,8,128]{4,3,2,1,0:T(8,128)S(1)} fusion(f32[4,128,16,64]{1,3,2,0:T(8,128)} %get-tuple-element.372, f32[4,16,64,128]{3,2,1,0:T(8,128)} %get-tuple-element.373, f32[16]{0:T(128)S(1)} %get-tuple-element.674, f32[4,128,16]{1,2,0:T(8,128)S(1)} %copy.94, f32[16,64,128]{2,1,0:T(8,128)S(1)} %get-tuple-element.377, ...), kind=kOutput, calls=%fused_computation.118 | convolution fusion | flops 138412032 | bytes 8028480 | tf_op jit(solution)/shard_map/btn,bhpn->bthp/dot_general | solution.py:94
  213.4 4.2 %rev.23 = f32[512,16,64]{0,2,1:T(8,128)} reverse(f32[512,16,64]{0,2,1:T(8,128)} %bitcast.294), dimensions={0} | reverse | bytes 4194304 | tf_op jit(solution)/shard_map/jit(_flip)/rev | solution.py:184
  217.6 9.1 %while.73 = (s32[]{:T(128)}, f32[16,64,128]{2,1,0:T(8,128)S(1)}, s32[]{:T(128)}, bf16[8,16]{1,0:T(8,128)(2,1)S(1)}, bf16[8,16,64,128]{3,2,1,0:T(8,128)(2,1)}, /*index=5*/s32[]{:T(128)}, s32[]{:T(128)}) while((s32[]{:T(128)}, f32[16,64,128]{2,1,0:T(8,128)S(1)}, s32[]{:T(128)}, bf16[8,16]{1,0:T(8,128)(2,1)S(1)}, ...), condition=%wide.region_4.5_spmd.clone, body=%wide.region_3.4_spmd.clone.sunk | while | flops 655380 | bytes 1310993 | solution.py:46
  226.7 3.3 %add_bitcast_fusion.1 = f32[4,16,8,8,128]{4,3,2,1,0:T(8,128)S(1)} fusion(f32[4,128,16,64]{1,3,2,0:T(8,128)} %get-tuple-element.365, f32[4,16,64,128]{3,2,1,0:T(8,128)} %get-tuple-element.366, f32[16]{0:T(128)S(1)} %get-tuple-element.673, f32[4,128,16]{1,2,0:T(8,128)S(1)} %copy.86, f32[16,64,128]{2,1,0:T(8,128)S(1)} %get-tuple-element.370, ...), kind=kOutput, calls=%fused_computation.121 | convolution fusion | flops 138412032 | bytes 8028480 | tf_op jit(solution)/shard_map/btn,bhpn->bthp/dot_general | solution.py:94
  230.3 3.2 %multiply_reduce_fusion = (f32[512]{0:T(512)S(1)}, f32[512,1024]{0,1:T(8,128)}) fusion(bf16[512,2592]{0,1:T(8,128)(2,1)} %bitcast.302, f32[512,16,64]{0,2,1:T(8,128)S(1)} %bitcast_add_fusion), kind=kLoop, calls=%fused_computation.117 | loop fusion | flops 4193792 | bytes 5244928 | tf_op jit(solution)/shard_map/reduce_sum | solution.py:187
  233.6 9.6 %psum.7 = f32[512]{0:T(512)S(1)} all-reduce(f32[512]{0:T(512)S(1)} %get-tuple-element.647), channel_id=1, replica_groups=mesh['frame'=8,'row'=4] {'row'}, use_global_device_ids=true, to_apply=%region_11.12 | all-reduce | flops 512 | bytes 4096 | tf_op jit(solution)/shard_map/psum | solution.py:188
  243.2 6.7 %fusion.58 = bf16[512,1,2048]{2,0,1:T(8,128)(2,1)} fusion(bf16[1024,2048]{1,0:T(8,128)(2,1)} %param.29, f32[512,1024]{0,1:T(8,128)} %get-tuple-element.648, f32[1024]{0:T(1024)S(1)} %copy-done.20, f32[512]{0:T(512)S(1)} %add_rsqrt_fusion), kind=kOutput, calls=%fused_computation.85 | convolution fusion | flops 2150105088 | bytes 8394752 | tf_op jit(solution)/shard_map/fpc,cd->fpd/dot_general | solution.py:192
  249.9 42.1 %reduce-scatter.2.cloned.1.call-done = bf16[128,1,2048]{2,0,1:T(8,128)(2,1)} async-done(((bf16[512,1,2048]{2,0,1:T(8,128)(2,1)}), bf16[128,1,2048]{2,0,1:T(8,128)(2,1)}) %reduce-scatter.2.cloned.1.call-update) | async-done | bytes 524304 | tf_op jit(solution)/shard_map/reduce_scatter | solution.py:193
  (269 shorter events, 116.2 us)
Async XLA Ops:
  6.5 58.6 %copy-start = (bf16[2048,512]{1,0:T(8,128)(2,1)S(1)}, bf16[2048,512]{1,0:T(8,128)(2,1)}, u32[]{:S(2)}) copy-start(bf16[2048,512]{1,0:T(8,128)(2,1)} %param.22) | copy-start | bytes 6291460
  6.5 50.8 %all-gather.8.cloned.1.call-start = ((), (), s32[]{:S(2)}) async-start(), calls=%async_computation.1 | async-start | bytes 2621440 | tf_op jit(solution)/shard_map/all_gather | solution.py:134
  7.3 192.1 %all-gather.12.cloned.1.call-start = ((), (), s32[]{:S(2)}) async-start(), calls=%async_computation.4 | async-start | bytes 2359296 | tf_op jit(solution)/shard_map/all_gather | solution.py:28
  57.3 5.4 %copy-start.2 = (bf16[1,512,2048]{2,1,0:T(8,128)(2,1)S(1)}, bf16[1,512,2048]{2,1,0:T(8,128)(2,1)}, u32[]{:S(2)}) copy-start(bf16[1,512,2048]{2,1,0:T(8,128)(2,1)} %all-gather.8.cloned.1.call-done) | copy-start | bytes 6291460
  57.3 5.4 %copy-start.19 = (bf16[2048,1024]{1,0:T(8,128)(2,1)S(1)}, bf16[2048,1024]{1,0:T(8,128)(2,1)}, u32[]{:S(2)}) copy-start(bf16[2048,1024]{1,0:T(8,128)(2,1)} %param.21) | copy-start | bytes 12582916
  67.7 8.6 %copy-start.3 = (bf16[1,512,2592]{1,2,0:T(8,128)(2,1)}, bf16[1,512,2592]{1,2,0:T(8,128)(2,1)S(1)}, u32[]{:S(2)}) copy-start(bf16[1,512,2592]{1,2,0:T(8,128)(2,1)S(1)} %fusion.115) | copy-start | bytes 7962628
  69.5 14.7 %collective-permute-start.1 = (bf16[3,1024]{0,1:T(8,128)(2,1)}, bf16[3,1024]{0,1:T(8,128)(2,1)}, u32[]{:S(2)}, u32[]{:S(2)}) collective-permute-start(bf16[3,1024]{0,1:T(8,128)(2,1)} %get-tuple-element.662), channel_id=1, source_target_pairs={{4,0},{8,4},{12,8},{16,12},{20,16},{24,20},{28,24},{5,1},{9,5},{13... | collective-permute-start | bytes 18440 | tf_op jit(solution)/shard_map/ppermute | solution.py:20
  70.8 13.4 %collective-permute-start = (bf16[3,1024]{0,1:T(8,128)(2,1)}, bf16[3,1024]{0,1:T(8,128)(2,1)}, u32[]{:S(2)}, u32[]{:S(2)}) collective-permute-start(bf16[3,1024]{0,1:T(8,128)(2,1)} %get-tuple-element.661), channel_id=1, source_target_pairs={{0,4},{4,8},{8,12},{12,16},{16,20},{20,24},{24,28},{1,5},{5,9},{9,... | collective-permute-start | bytes 18440 | tf_op jit(solution)/shard_map/ppermute | solution.py:19
  79.1 3.3 %copy-start.7 = (bf16[4,128,128]{1,0,2:T(4,128)(2,1)}, bf16[4,128,128]{1,0,2:T(4,128)(2,1)S(1)}, u32[]{:S(2)}) copy-start(bf16[4,128,128]{1,0,2:T(4,128)(2,1)S(1)} %reshape.213) | copy-start | bytes 393220
  83.4 2.8 copy-start.5
  84.2 2.0 copy-start.13
  84.2 2.0 copy-start.14
  84.2 2.0 copy-start.15
  152.9 64.7 %all-gather.10.cloned.1.call-start = ((), (), s32[]{:S(2)}) async-start(), calls=%async_computation.3 | async-start | bytes 2359296 | tf_op jit(solution)/shard_map/all_gather | solution.py:28
  152.9 3.3 %copy-start.4 = (bf16[512,128]{1,0:T(8,128)(2,1)S(1)}, bf16[512,128]{1,0:T(8,128)(2,1)}, u32[]{:S(2)}) copy-start(bf16[512,128]{1,0:T(8,128)(2,1)} %copy.102) | copy-start | bytes 393220
  153.0 3.3 %copy-start.11 = (f32[1,16]{1,0:T(1,128)S(1)}, f32[1,16]{1,0:T(1,128)}, u32[]{:S(2)}) copy-start(f32[1,16]{1,0:T(1,128)} %get-tuple-element.952) | copy-start | bytes 196
  153.0 3.3 %copy-start.16 = (f32[16]{0:T(128)S(1)}, f32[16]{0:T(128)}, u32[]{:S(2)}) copy-start(f32[16]{0:T(128)} %custom-call.1) | copy-start | bytes 196
  156.3 26.2 %copy-start.18 = (f32[2,16]{1,0:T(2,128)S(1)}, f32[2,16]{1,0:T(2,128)}, u32[]{:S(2)}) copy-start(f32[2,16]{1,0:T(2,128)} %param.27) | copy-start | bytes 388
  156.3 41.9 %copy-start.17 = (f32[4,16]{1,0:T(4,128)S(1)}, f32[4,16]{1,0:T(4,128)}, u32[]{:S(2)}) copy-start(f32[4,16]{1,0:T(4,128)} %get-tuple-element.374) | copy-start | bytes 772
  180.4 111.6 %reduce-scatter.2.cloned.1.call-start = ((), (), s32[]{:S(2)}) async-start(), calls=%async_computation.2 | async-start | bytes 2621440 | tf_op jit(solution)/shard_map/reduce_scatter | solution.py:193
  199.4 9.2 %copy-start.8 = (bf16[4,128,128]{1,0,2:T(4,128)(2,1)S(1)}, bf16[4,128,128]{1,0,2:T(4,128)(2,1)}, u32[]{:S(2)}) copy-start(bf16[4,128,128]{1,0,2:T(4,128)(2,1)} %copy-done.7) | copy-start | bytes 393220
  217.6 9.1 %copy-start.6 = (bf16[4,128,128]{1,0,2:T(4,128)(2,1)S(1)}, bf16[4,128,128]{1,0,2:T(4,128)(2,1)}, u32[]{:S(2)}) copy-start(bf16[4,128,128]{1,0,2:T(4,128)(2,1)} %copy-done.5) | copy-start | bytes 393220
  226.7 3.3 %copy-start.1 = (f32[512,16,64]{0,2,1:T(8,128)S(1)}, f32[512,16,64]{0,2,1:T(8,128)}, u32[]{:S(2)}) copy-start(f32[512,16,64]{0,2,1:T(8,128)} %rev.23) | copy-start | bytes 6291460
  230.3 12.9 %copy-start.20 = (f32[1024]{0:T(1024)S(1)}, f32[1024]{0:T(1024)}, u32[]{:S(2)}) copy-start(f32[1024]{0:T(1024)} %param.28) | copy-start | bytes 12292
  (3 other events, 4.2 us)
Sparse Core Ops, SparseCore 0:
  8.9 48.3 all-gather.7
  153.0 26.8 all-gather.11
  181.8 27.8 all-gather.9
  250.0 41.9 reduce-scatter.1
where the time goes:
time: 302 us; the launch traced here: 299 us
  waiting for transfers between devices  89.3 us (30%)
  matrix products  58.9 us (20%)
  local copies, waits for them, and re-layouts  55.5 us (18%)
  other arithmetic  51.7 us (17%)
  blocking collectives  23 us (8%)
  between operations  14.2 us (5%)
  starting transfers between devices  5.15 us (2%)
    all_gather x1, waiting for transfers between devices, per_device(): shard_piece = lax.all_gather(tokens, 'row', axis=1, tiled=True)  46.3 us
    reduce_scatter x1, waiting for transfers between devices, per_device(): lax.psum_scatter(jnp.transpose(partial_value, (1, 0, 2)).astype(jnp.bfloa...  42.1 us
    dot_general x8, matrix products, advance(): jnp.einsum('hts,shp->thp', weights, x_block, preferred_element_type=jnp.f...  18.6 us
    select_n x16, other arithmetic, lap(): return jax.tree.map(lambda a, b: jnp.where(reached, a, b), new, before)  17.5 us
    unnamed x1, blocking collectives  13.4 us
    unnamed x55, local copies, waits for them, and re-layouts  12.5 us
    dot_general x5, matrix products, per_device(): jnp.einsum('frd,dk->frk', shard_piece, matrix, preferred_element_type=jnp...  10.4 us
    psum x1, blocking collectives, per_device(): total_squares = lax.psum(local_squares, 'row')  9.61 us
  transfers between devices with their start and end apart: 6, of which 2 were waited for; matrix products, arithmetic and copies ran while one was open for 21% of the time, Pallas kernels for 0%

commit v1 on v0

--- a/solution.py
+++ b/solution.py
@@ -131,7 +131,12 @@
     channels = w_gate.shape[1]
     heads_here = step_bias.shape[1]
     state_size = w_state_proj.shape[1] // 4
-    shard_piece = lax.all_gather(tokens, "row", axis=1, tiled=True)
+    ring = [tokens]
+    for hop in range(3):
+        ring.append(lax.ppermute(ring[-1], "row", [(dev, (dev + 1) % 4) for dev in range(4)]))
+    shard_piece = jnp.roll(
+        jnp.concatenate(ring[::-1], axis=1), (lax.axis_index("row") + 1) * ring[0].shape[1], axis=1
+    )
     matrices = (w_gate, w_value, w_state_proj, w_step[0], w_step[1])
     outputs = [
         jnp.einsum("frd,dk->frk", shard_piece, matrix, preferred_element_type=jnp.float32).astype(

time: 302 us -> 260 us (0.86)
  local copies, waits for them, and re-layouts: 55.5 us -> 38.3 us
  other arithmetic: 51.7 us -> 39.2 us
  matrix products: 58.9 us -> 52.6 us
  waiting for transfers between devices: 89.3 us -> 83.2 us
  starting transfers between devices: 5.15 us -> 8.18 us
    all_gather x1 -> x0, waiting for transfers between devices: 46.3 us -> none  [per_device(): shard_piece = lax.all_gather(tokens, 'row', axis=1, tiled=True)]
    ppermute x0 -> x3, waiting for transfers between devices: none -> 40.3 us  [per_device(): lax.ppermute(ring[-1], 'row', [(dev, (dev + 1) % 4) for dev in range(4)])]
    dynamic_update_slice x16, local copies, waits for them, and re-layouts: 7.74 us -> 0.38 us  [local_pass(): lax.scan(advance, (state_zero, jnp.zeros((heads_here,), jnp.float32)), bl...]
    add x8, other arithmetic: 4.33 us -> 0.1 us  [advance(): offset + log_last]
    transpose x16, local copies, waits for them, and re-layouts: 3.88 us -> 0.51 us  [block_weights(): return (scores[None] * fading * dt_block.T[:, None, :]).astype(jnp.bfloat16)]
    mul x8, other arithmetic: 3.42 us -> 0.06 us  [advance(): log_cum = jnp.cumsum(-dt_block * rate_row[None, :], axis=0)]
    mul x8, other arithmetic: 3.53 us -> 0.18 us  [advance(): jnp.exp(log_last[None, :] - log_cum) * dt_block]
    dot_general x8, matrix products: 7.37 us -> 4.22 us  [advance(): jnp.einsum('tn,sn->ts', c_block, b_block, preferred_element_type=jnp.floa...]
  transfers between devices with their start and end apart: 6 -> 8, of which waited for: 2 -> 4; matrix products, arithmetic and copies ran while one was open for 21% -> 21% of each run, Pallas kernels for 0% -> 0%
where the time goes in v1:
time: 260 us; the launch traced here: 258 us
  waiting for transfers between devices  83.2 us (32%)
  matrix products  52.6 us (20%)
  other arithmetic  39.2 us (15%)
  local copies, waits for them, and re-layouts  38.3 us (15%)
  blocking collectives  21.4 us (8%)
  between operations  14.3 us (6%)
  starting transfers between devices  8.18 us (3%)
    reduce_scatter x1, waiting for transfers between devices, per_device(): lax.psum_scatter(jnp.transpose(partial_value, (1, 0, 2)).astype(jnp.bfloa...  42.8 us
    ppermute x3, waiting for transfers between devices, per_device(): lax.ppermute(ring[-1], 'row', [(dev, (dev + 1) % 4) for dev in range(4)])  40.3 us
    dot_general x8, matrix products, advance(): jnp.einsum('hts,shp->thp', weights, x_block, preferred_element_type=jnp.f...  18.7 us
    select_n x16, other arithmetic, lap(): return jax.tree.map(lambda a, b: jnp.where(reached, a, b), new, before)  17.6 us
    unnamed x1, blocking collectives  13 us
    unnamed x76, local copies, waits for them, and re-layouts  12.1 us
    dot_general x8, matrix products, advance(): jnp.einsum('sn,shp->hpn', b_block, carried, preferred_element_type=jnp.fl...  9.57 us
    psum x1, blocking collectives, per_device(): total_squares = lax.psum(local_squares, 'row')  8.34 us
  transfers between devices with their start and end apart: 8, of which 4 were waited for; matrix products, arithmetic and copies ran while one was open for 21% of the time, Pallas kernels for 0%

profile of v1, /device:TPU:0, one launch (start us, length us, event | category | flops | bytes accessed | tf_op | source)
XLA Modules:
  0.0 258.2 jit_solution(3260966323146290923)
XLA Ops:
  6.5 3.1 %collective-permute-start = (bf16[1,128,2048]{2,1,0:T(8,128)(2,1)}, bf16[1,128,2048]{2,1,0:T(8,128)(2,1)S(1)}, u32[]{:S(2)}, u32[]{:S(2)}) collective-permute-start(bf16[1,128,2048]{2,1,0:T(8,128)(2,1)} %param.19), channel_id=1, source_target_pairs={{0,1},{1,2},{2,3},{3,0},{4,5},{5,6},{6,7},{7,4},{8,9},{9,10},{10,1... | collective-permute-start | bytes 1572872 | tf_op jit(solution)/shard_map/ppermute | solution.py:136
  9.6 14.2 %collective-permute-done = bf16[1,128,2048]{2,1,0:T(8,128)(2,1)S(1)} collective-permute-done((bf16[1,128,2048]{2,1,0:T(8,128)(2,1)}, bf16[1,128,2048]{2,1,0:T(8,128)(2,1)S(1)}, u32[]{:S(2)}, u32[]{:S(2)}) %collective-permute-start) | collective-permute-done | bytes 524320 | tf_op jit(solution)/shard_map/ppermute | solution.py:136
  23.8 15.0 %collective-permute-done.1 = bf16[1,128,2048]{2,1,0:T(8,128)(2,1)} collective-permute-done((bf16[1,128,2048]{2,1,0:T(8,128)(2,1)S(1)}, bf16[1,128,2048]{2,1,0:T(8,128)(2,1)}, u32[]{:S(2)}, u32[]{:S(2)}) %collective-permute-start.1) | collective-permute-done | bytes 524320 | tf_op jit(solution)/shard_map/ppermute | solution.py:136
  41.9 11.2 %collective-permute-done.2 = bf16[1,128,2048]{2,1,0:T(8,128)(2,1)} collective-permute-done((bf16[1,128,2048]{2,1,0:T(8,128)(2,1)}, bf16[1,128,2048]{2,1,0:T(8,128)(2,1)}, u32[]{:S(2)}, u32[]{:S(2)}) %collective-permute-start.2) | collective-permute-done | bytes 524320 | tf_op jit(solution)/shard_map/ppermute | solution.py:136
  58.0 2.4 fusion.94
  60.4 2.4 fusion.88
  68.4 3.8 %collective-permute-start.3 = (bf16[3,1024]{0,1:T(8,128)(2,1)}, bf16[3,1024]{0,1:T(8,128)(2,1)}, u32[]{:S(2)}, u32[]{:S(2)}) collective-permute-start(bf16[3,1024]{0,1:T(8,128)(2,1)} %get-tuple-element.661), channel_id=1, source_target_pairs={{0,4},{4,8},{8,12},{12,16},{16,20},{20,24},{24,28},{1,5},{5,9},{9,... | collective-permute-start | bytes 18440 | tf_op jit(solution)/shard_map/ppermute | solution.py:19
  77.8 5.7 %multiply_convert_fusion.8 = (bf16[512,1024]{0,1:T(8,128)(2,1)}, bf16[512,1024]{0,1:T(8,128)(2,1)}) fusion(f32[518,1024]{0,1:T(8,128)S(1)} %maximum_convert_fusion, f32[1024]{0:T(1024)S(1)} %bitcast.314, f32[1024]{0:T(1024)S(1)} %bitcast.315, f32[1024]{0:T(1024)S(1)} %bitcast.316, f32[1024]{0:T(1024)S(1)} %bitcast.311, f32[1024]{0:T(1024)S(1)} %bitcast.317, ...), kind=kLoop, calls=%fused_computation.123 | loop fusion | flops 12582912 | bytes 16809984 | tf_op jit(solution)/shard_map/convert_element_type | solution.py:115
  83.5 2.5 rev.20
  90.5 20.3 %while.74 = (s32[]{:T(128)}, f32[16,64,128]{2,1,0:T(8,128)S(1)}, f32[16]{0:T(128)S(1)}, f32[4,128,16,64]{1,3,2,0:T(8,128)}, f32[4,128,16]{2,1,0:T(8,128)S(1)}, /...) while((s32[]{:T(128)}, f32[16,64,128]{2,1,0:T(8,128)S(1)}, ...), condition=%wide.region_7.8_spmd.clone, body=%wide.region_5.7_spmd.clone.sunk | while | flops 73816096 | bytes 3699580 | solution.py:86
  98.2 2.4 fusion.195
  103.3 2.4 fusion.195
  108.4 2.4 fusion.195
  118.3 23.3 %while.72 = (s32[]{:T(128)}, f32[16,64,128]{2,1,0:T(8,128)S(1)}, f32[16]{0:T(128)S(1)}, f32[4,128,16,64]{1,3,2,0:T(8,128)}, f32[4,128,16]{2,1,0:T(8,128)S(1)}, /...) while((s32[]{:T(128)}, f32[16,64,128]{2,1,0:T(8,128)S(1)}, ...), condition=%wide.region_2.3_spmd.clone, body=%wide.region_0.2_spmd.clone.sunk | while | flops 73816096 | bytes 3699580 | solution.py:86
  145.7 13.0 %all-reduce.2 = (bf16[128]{0:T(256)(128)(2,1)S(1)}, bf16[128]{0:T(256)(128)(2,1)S(1)}) all-reduce(bf16[128]{0:T(256)(128)(2,1)S(1)} %dynamic-update-slice.1, bf16[128]{0:T(256)(128)(2,1)S(1)} %dynamic-update-slice), channel_id=4, replica_groups=mesh['frame'=8,'row'=4] {'frame'}, use_global_device_ids=true, to_apply=%add.1 | all-reduce | flops 256 | bytes 1024
  159.8 9.2 %while.75 = (s32[]{:T(128)}, f32[16,64,128]{2,1,0:T(8,128)S(1)}, s32[]{:T(128)}, bf16[8,16]{1,0:T(8,128)(2,1)S(1)}, bf16[8,16,64,128]{3,2,1,0:T(8,128)(2,1)}, /*index=5*/s32[]{:T(128)}, s32[]{:T(128)}, s32[]{:T(128)}, s32[]{:T(128)}) while((s32[]{:T(128)}, f32[16,64,128]{2,1,0:T(8,128)S(1)}, s32[]{:T(128)}, ...), condition=%wide.region_9.10_spmd.clone, body=%wide.region_8.9_spmd.clone.sunk | while | flops 655384 | bytes 1311055 | solution.py:46
  169.0 2.9 %add_bitcast_fusion = f32[4,16,8,8,128]{4,3,2,1,0:T(8,128)S(1)} fusion(f32[4,128,16,64]{1,3,2,0:T(8,128)} %get-tuple-element.372, f32[4,16,64,128]{3,2,1,0:T(8,128)} %get-tuple-element.373, f32[16]{0:T(128)S(1)} %get-tuple-element.674, f32[4,128,16]{1,2,0:T(8,128)S(1)} %copy.94, f32[16,64,128]{2,1,0:T(8,128)S(1)} %get-tuple-element.377, ...), kind=kOutput, calls=%fused_computation.118 | convolution fusion | flops 138412032 | bytes 8028480 | tf_op jit(solution)/shard_map/btn,bhpn->bthp/dot_general | solution.py:94
  173.6 4.2 %rev.23 = f32[512,16,64]{0,2,1:T(8,128)} reverse(f32[512,16,64]{0,2,1:T(8,128)} %bitcast.294), dimensions={0} | reverse | bytes 4194304 | tf_op jit(solution)/shard_map/jit(_flip)/rev | solution.py:189
  177.8 9.2 %while.73 = (s32[]{:T(128)}, f32[16,64,128]{2,1,0:T(8,128)S(1)}, s32[]{:T(128)}, bf16[8,16]{1,0:T(8,128)(2,1)S(1)}, bf16[8,16,64,128]{3,2,1,0:T(8,128)(2,1)}, /*index=5*/s32[]{:T(128)}, s32[]{:T(128)}) while((s32[]{:T(128)}, f32[16,64,128]{2,1,0:T(8,128)S(1)}, s32[]{:T(128)}, bf16[8,16]{1,0:T(8,128)(2,1)S(1)}, ...), condition=%wide.region_4.5_spmd.clone, body=%wide.region_3.4_spmd.clone.sunk | while | flops 655380 | bytes 1310993 | solution.py:46
  187.1 3.0 %add_bitcast_fusion.1 = f32[4,16,8,8,128]{4,3,2,1,0:T(8,128)S(1)} fusion(f32[4,128,16,64]{1,3,2,0:T(8,128)} %get-tuple-element.365, f32[4,16,64,128]{3,2,1,0:T(8,128)} %get-tuple-element.366, f32[16]{0:T(128)S(1)} %get-tuple-element.673, f32[4,128,16]{1,2,0:T(8,128)S(1)} %copy.86, f32[16,64,128]{2,1,0:T(8,128)S(1)} %get-tuple-element.370, ...), kind=kOutput, calls=%fused_computation.121 | convolution fusion | flops 138412032 | bytes 8028480 | tf_op jit(solution)/shard_map/btn,bhpn->bthp/dot_general | solution.py:94
  190.4 3.2 %multiply_reduce_fusion = (f32[512]{0:T(512)S(1)}, f32[512,1024]{0,1:T(8,128)}) fusion(bf16[512,2592]{0,1:T(8,128)(2,1)} %bitcast.302, f32[512,16,64]{0,2,1:T(8,128)S(1)} %bitcast_add_fusion), kind=kLoop, calls=%fused_computation.117 | loop fusion | flops 4193792 | bytes 5244928 | tf_op jit(solution)/shard_map/reduce_sum | solution.py:192
  193.6 8.3 %psum.7 = f32[512]{0:T(512)S(1)} all-reduce(f32[512]{0:T(512)S(1)} %get-tuple-element.647), channel_id=1, replica_groups=mesh['frame'=8,'row'=4] {'row'}, use_global_device_ids=true, to_apply=%region_11.12 | all-reduce | flops 512 | bytes 4096 | tf_op jit(solution)/shard_map/psum | solution.py:193
  202.0 6.8 %fusion.58 = bf16[512,1,2048]{2,0,1:T(8,128)(2,1)} fusion(bf16[1024,2048]{1,0:T(8,128)(2,1)} %param.29, f32[512,1024]{0,1:T(8,128)} %get-tuple-element.648, f32[1024]{0:T(1024)S(1)} %copy-done.27, f32[512]{0:T(512)S(1)} %add_rsqrt_fusion), kind=kOutput, calls=%fused_computation.85 | convolution fusion | flops 2150105088 | bytes 8394752 | tf_op jit(solution)/shard_map/fpc,cd->fpd/dot_general | solution.py:197
  208.8 42.8 %reduce-scatter.2.cloned.1.call-done = bf16[128,1,2048]{2,0,1:T(8,128)(2,1)} async-done(((bf16[512,1,2048]{2,0,1:T(8,128)(2,1)}), bf16[128,1,2048]{2,0,1:T(8,128)(2,1)}) %reduce-scatter.2.cloned.1.call-update) | async-done | bytes 524304 | tf_op jit(solution)/shard_map/reduce_scatter | solution.py:198
  (294 shorter events, 91.3 us)
Async XLA Ops:
  6.5 56.2 %copy-start = (bf16[2048,512]{1,0:T(8,128)(2,1)S(1)}, bf16[2048,512]{1,0:T(8,128)(2,1)}, u32[]{:S(2)}) copy-start(bf16[2048,512]{1,0:T(8,128)(2,1)} %param.22) | copy-start | bytes 6291460
  6.5 153.3 %all-gather.9.cloned.1.call-start = ((), (), s32[]{:S(2)}) async-start(), calls=%async_computation.3 | async-start | bytes 2359296 | tf_op jit(solution)/shard_map/all_gather | solution.py:28
  6.5 17.2 %collective-permute-start = (bf16[1,128,2048]{2,1,0:T(8,128)(2,1)}, bf16[1,128,2048]{2,1,0:T(8,128)(2,1)S(1)}, u32[]{:S(2)}, u32[]{:S(2)}) collective-permute-start(bf16[1,128,2048]{2,1,0:T(8,128)(2,1)} %param.19), channel_id=1, source_target_pairs={{0,1},{1,2},{2,3},{3,0},{4,5},{5,6},{6,7},{7,4},{8,9},{9,10},{10,1... | collective-permute-start | bytes 1572872 | tf_op jit(solution)/shard_map/ppermute | solution.py:136
  23.7 15.8 %copy-start.7 = (bf16[1,128,2048]{2,1,0:T(8,128)(2,1)}, bf16[1,128,2048]{2,1,0:T(8,128)(2,1)S(1)}, u32[]{:S(2)}) copy-start(bf16[1,128,2048]{2,1,0:T(8,128)(2,1)S(1)} %collective-permute-done) | copy-start | bytes 1572868
  23.8 15.0 %collective-permute-start.1 = (bf16[1,128,2048]{2,1,0:T(8,128)(2,1)S(1)}, bf16[1,128,2048]{2,1,0:T(8,128)(2,1)}, u32[]{:S(2)}, u32[]{:S(2)}) collective-permute-start(bf16[1,128,2048]{2,1,0:T(8,128)(2,1)S(1)} %collective-permute-done), channel_id=1, source_target_pairs={{0,1},{1,2},{2,3},{3,0},{4,5},{5,6},{6,7},{7,4},{8,9},{9,10},{10,1... | collective-permute-start | bytes 1572872 | tf_op jit(solution)/shard_map/ppermute | solution.py:136
  38.7 14.3 %collective-permute-start.2 = (bf16[1,128,2048]{2,1,0:T(8,128)(2,1)}, bf16[1,128,2048]{2,1,0:T(8,128)(2,1)}, u32[]{:S(2)}, u32[]{:S(2)}) collective-permute-start(bf16[1,128,2048]{2,1,0:T(8,128)(2,1)} %collective-permute-done.1), channel_id=1, source_target_pairs={{0,1},{1,2},{2,3},{3,0},{4,5},{5,6},{6,7},{7,4},{8,9},{9,10},{10,1... | collective-permute-start | bytes 1572872 | tf_op jit(solution)/shard_map/ppermute | solution.py:136
  39.5 15.7 %copy-start.8 = (bf16[1,128,2048]{2,1,0:T(8,128)(2,1)S(1)}, bf16[1,128,2048]{2,1,0:T(8,128)(2,1)}, u32[]{:S(2)}) copy-start(bf16[1,128,2048]{2,1,0:T(8,128)(2,1)} %copy-done.7) | copy-start | bytes 1572868
  39.5 15.8 %copy-start.6 = (bf16[1,128,2048]{2,1,0:T(8,128)(2,1)S(1)}, bf16[1,128,2048]{2,1,0:T(8,128)(2,1)}, u32[]{:S(2)}) copy-start(bf16[1,128,2048]{2,1,0:T(8,128)(2,1)} %param.19) | copy-start | bytes 1572868
  55.3 2.6 %copy-start.25 = (bf16[2048,1024]{1,0:T(8,128)(2,1)S(1)}, bf16[2048,1024]{1,0:T(8,128)(2,1)}, u32[]{:S(2)}) copy-start(bf16[2048,1024]{1,0:T(8,128)(2,1)} %param.20) | copy-start | bytes 12582916
  65.4 6.9 %copy-start.5 = (bf16[1,512,2592]{1,2,0:T(8,128)(2,1)}, bf16[1,512,2592]{1,2,0:T(8,128)(2,1)S(1)}, u32[]{:S(2)}) copy-start(bf16[1,512,2592]{1,2,0:T(8,128)(2,1)S(1)} %fusion.115) | copy-start | bytes 7962628
  67.1 8.9 %collective-permute-start.4 = (bf16[3,1024]{0,1:T(8,128)(2,1)}, bf16[3,1024]{0,1:T(8,128)(2,1)}, u32[]{:S(2)}, u32[]{:S(2)}) collective-permute-start(bf16[3,1024]{0,1:T(8,128)(2,1)} %get-tuple-element.662), channel_id=1, source_target_pairs={{4,0},{8,4},{12,8},{16,12},{20,16},{24,20},{28,24},{5,1},{9,5},{13... | collective-permute-start | bytes 18440 | tf_op jit(solution)/shard_map/ppermute | solution.py:20
  68.4 7.6 %collective-permute-start.3 = (bf16[3,1024]{0,1:T(8,128)(2,1)}, bf16[3,1024]{0,1:T(8,128)(2,1)}, u32[]{:S(2)}, u32[]{:S(2)}) collective-permute-start(bf16[3,1024]{0,1:T(8,128)(2,1)} %get-tuple-element.661), channel_id=1, source_target_pairs={{0,4},{4,8},{8,12},{12,16},{16,20},{20,24},{24,28},{1,5},{5,9},{9,... | collective-permute-start | bytes 18440 | tf_op jit(solution)/shard_map/ppermute | solution.py:19
  87.2 3.3 %copy-start.23 = (f32[16]{0:T(128)S(1)}, f32[16]{0:T(128)}, u32[]{:S(2)}) copy-start(f32[16]{0:T(128)} %custom-call.4) | copy-start | bytes 196
  112.9 3.9 %copy-start.2 = (bf16[4,128,16,64]{1,0,3,2:T(4,128)(2,1)}, bf16[4,128,16,64]{1,0,3,2:T(4,128)(2,1)S(1)}, u32[]{:S(2)}) copy-start(bf16[4,128,16,64]{1,0,3,2:T(4,128)(2,1)S(1)} %reshape_reshape.3) | copy-start | bytes 3145732
  115.0 62.8 %all-gather.7.cloned.1.call-start = ((), (), s32[]{:S(2)}) async-start(), calls=%async_computation.2 | async-start | bytes 2359296 | tf_op jit(solution)/shard_map/all_gather | solution.py:28
  115.0 3.3 %copy-start.22 = (f32[16]{0:T(128)S(1)}, f32[16]{0:T(128)}, u32[]{:S(2)}) copy-start(f32[16]{0:T(128)} %custom-call.1) | copy-start | bytes 196
  118.3 26.8 %copy-start.14 = (f32[4,128,16]{2,1,0:T(8,128)S(1)}, f32[4,128,16]{2,1,0:T(8,128)}, u32[]{:S(2)}) copy-start(f32[4,128,16]{2,1,0:T(8,128)} %copy-done.13) | copy-start | bytes 98308
  142.4 109.2 %reduce-scatter.2.cloned.1.call-start = ((), (), s32[]{:S(2)}) async-start(), calls=%async_computation.1 | async-start | bytes 2621440 | tf_op jit(solution)/shard_map/reduce_scatter | solution.py:198
  159.8 9.2 %copy-start.12 = (bf16[4,128,128]{1,0,2:T(4,128)(2,1)S(1)}, bf16[4,128,128]{1,0,2:T(4,128)(2,1)}, u32[]{:S(2)}) copy-start(bf16[4,128,128]{1,0,2:T(4,128)(2,1)} %copy-done.11) | copy-start | bytes 393220
  177.8 9.2 %copy-start.3 = (bf16[4,128,16,64]{1,0,3,2:T(4,128)(2,1)S(1)}, bf16[4,128,16,64]{1,0,3,2:T(4,128)(2,1)}, u32[]{:S(2)}) copy-start(bf16[4,128,16,64]{1,0,3,2:T(4,128)(2,1)} %copy-done.2) | copy-start | bytes 3145732
  177.8 9.2 %copy-start.10 = (bf16[4,128,128]{1,0,2:T(4,128)(2,1)S(1)}, bf16[4,128,128]{1,0,2:T(4,128)(2,1)}, u32[]{:S(2)}) copy-start(bf16[4,128,128]{1,0,2:T(4,128)(2,1)} %copy-done.9) | copy-start | bytes 393220
  187.1 3.0 %copy-start.4 = (f32[512,16,64]{0,2,1:T(8,128)S(1)}, f32[512,16,64]{0,2,1:T(8,128)}, u32[]{:S(2)}) copy-start(f32[512,16,64]{0,2,1:T(8,128)} %rev.23) | copy-start | bytes 6291460
  190.4 11.6 %copy-start.27 = (f32[1024]{0:T(1024)S(1)}, f32[1024]{0:T(1024)}, u32[]{:S(2)}) copy-start(f32[1024]{0:T(1024)} %param.28) | copy-start | bytes 12292
  202.0 49.7 %copy-start.1 = (bf16[2048,512]{1,0:T(8,128)(2,1)S(1)}, bf16[2048,512]{1,0:T(8,128)(2,1)}, u32[]{:S(2)}) copy-start(bf16[2048,512]{1,0:T(8,128)(2,1)} %param.22) | copy-start | bytes 6291460
  (12 other events, 19.4 us)
Sparse Core Ops, SparseCore 0:
  115.1 26.5 all-gather.8
  143.6 27.7 all-gather.6
  209.0 42.6 reduce-scatter.1
